TPU v7x, 256 devices: a whole 4x4x8 slice. The times are simulated.
256 devices in a mesh: row: 128 (over y, x, z), col: 2 (over core).
Axes of the slice: x: 4, y: 4, z: 8, core: 2. Of those that a mesh axis runs over, the one named last changes fastest.
Arguments:
- features: float32 [64, 32768], P(None, ('row', 'col')), may hold values from -12 to 12
- initial: float32 [32768], P(('row', 'col')), may hold values from 0.1 to 90, as said below
Outputs:
- dist: float32 [32768], P(('row', 'col'))
- residuals: float32 [2], replicated
Inputs may be any that keep to these rules, and one draw needn't show every extreme that they name: `initial`: positive starting weights of the policies.
All inputs are finite; a program needn't handle non-finite values.
Results may differ from a plain program's by a relative error of at most 0.0003.
Values sent between devices are 32-bit elements; how exact they have to be, the bound alone decides.
No kernel may reach another device: no remote copies, remote signals or barrier semaphores. Data moves between devices by JAX's collectives and lax.ppermute only.
A program may use at most 64 MiB of HBM per device.

v0:
```python
import functools
import math
import jax
import jax.numpy as jnp
from jax import lax
from jax.sharding import Mesh
from jax.sharding import PartitionSpec as P

NPOL = 32768
ITERS = 2
ROW_COL = ("row_0", "row_1", "row_2", "col")
ROW = ("row_0", "row_1", "row_2")
intensity = 0.25
column_block = 2048


def in_order(blocks, dim):
    lengths = list(blocks.shape[1:])
    lengths[dim] *= blocks.shape[0]
    return jnp.moveaxis(blocks, 0, dim).reshape(lengths)


def copy_for_each(array, axis):
    copies = jnp.broadcast_to(array, (lax.axis_size(axis), *array.shape))
    return lax.all_to_all(copies, axis, split_axis=0, concat_axis=0, tiled=True)


def gathered_copies(array, axis, dim):
    return in_order(copy_for_each(array, axis), dim)


def one_axis_at_a_time(array, axes):
    return functools.reduce(lax.psum, axes, array)


def all_blocks(array, axes, turns):
    blocks = array[None]
    for k in turns:
        blocks = lax.all_gather(blocks, axes[k], axis=0, tiled=True)
    block = [lax.axis_size(axes[k]) for k in reversed(turns)]
    blocks = blocks.reshape(*block, *array.shape)
    turned = sorted(range(len(turns)), key=lambda place: turns[len(turns) - 1 - place])
    return blocks.transpose(*turned, *range(len(turns), blocks.ndim)).reshape(-1, *array.shape)


def gathered_by_axis(array, axes, turns, dim):
    return in_order(all_blocks(array, axes, turns), dim)


def cut_along(array, dim, count):
    lengths = array.shape
    blocks = array.reshape(*lengths[:dim], count, lengths[dim] // count, *lengths[dim + 1 :])
    return jnp.moveaxis(blocks, dim, 0)


def sum_at_owner(array, axis, dim):
    blocks = cut_along(array, dim, lax.axis_size(axis))
    arrived = lax.all_to_all(blocks, axis, split_axis=0, concat_axis=0, tiled=True)
    return arrived.sum(axis=0)


def sum_in_two_steps(array, axes, dim):
    far, near = axes
    blocks = cut_along(array, dim, lax.axis_size(far))
    nearer = sum_at_owner(blocks, near, dim + 1)
    arrived = lax.all_to_all(nearer, far, split_axis=0, concat_axis=0, tiled=True)
    return arrived.sum(axis=0)


def of_everyone(array, axis):
    everything = copy_for_each(array, axis)
    return jnp.sum(everything, axis=0)


def by_axis(array, axes):
    far, near = axes
    nearer = of_everyone(array, near)
    return of_everyone(nearer, far)


def in_one(arrays, axis):
    line, at, done = (jnp.concatenate([a.reshape(-1) for a in arrays]), 0, [])
    total = by_axis(line, axis)
    for a in arrays:
        done.append(total[at : at + a.size].reshape(a.shape))
        at += a.size
    return tuple(done)


def column_pass(row_side, rows_mass, column_feats):
    columns = column_feats.shape[1]
    block_width = math.gcd(columns, column_block)
    count_blocks = columns // block_width

    def one_block(block_index):
        segment = lax.dynamic_slice_in_dim(column_feats, block_index * block_width, block_width, 1)
        payoff = jnp.einsum("kr,kc->rc", row_side, segment, precision=lax.Precision.HIGHEST)
        moves = jax.nn.sigmoid(intensity * payoff)
        inflow = jnp.dot(rows_mass, moves, precision=lax.Precision.HIGHEST)
        return (inflow, jnp.sum(moves, axis=1))

    inflows, totals = lax.map(one_block, jnp.arange(count_blocks, dtype=jnp.int32))
    return (inflows.reshape(columns), jnp.sum(totals, axis=0))


def on_device(features, initial):
    half_feat = features.shape[0] // 2
    row_feats = gathered_copies(features, "col", 1)
    row_side = jnp.concatenate([row_feats[half_feat:], -row_feats[:half_feat]], axis=0)
    step_rate = 1.0 / NPOL
    weights = initial / one_axis_at_a_time(jnp.sum(initial), ROW_COL)
    column_feats = gathered_by_axis(features, ROW, (0, 1, 2), 1)
    changes = []
    pending = jnp.zeros((), jnp.float32)
    own_totals = jnp.zeros_like(weights)
    for iteration in range(ITERS):
        rows_mass = gathered_copies(weights, "col", 0)
        inflow, totals = column_pass(row_side, rows_mass, column_feats)
        if iteration == 0:
            own_totals = sum_at_owner(totals, "col", 0)
        summed = sum_in_two_steps(inflow, ("row_0", ("row_1", "row_2")), 0)
        advanced = step_rate * summed + weights * (1.0 - step_rate * own_totals)
        normalizer, earlier = in_one(
            (jnp.sum(advanced), pending), ("row_0", ("row_1", "row_2", "col"))
        )
        if iteration > 0:
            changes.append(earlier)
        updated = advanced / normalizer
        pending = jnp.sum(jnp.abs(updated - weights))
        weights = updated
    changes.append(one_axis_at_a_time(pending, ROW_COL))
    return (NPOL * weights, jnp.stack(changes))


def solution(mesh):
    torus = Mesh(
        mesh.devices.reshape(4, 4, 8, mesh.shape["col"]), ("row_0", "row_1", "row_2", "col")
    )
    in_specs = (P(None, ROW_COL), P(ROW_COL))
    out_specs = (P(ROW_COL), P())
    return jax.shard_map(
        on_device, mesh=torus, in_specs=in_specs, out_specs=out_specs, check_vma=False
    )
```

profile of v0, /device:TPU:1, one launch (start us, length us, event | category | flops | bytes accessed | tf_op | source)
XLA Modules:
  0.0 353.5 jit_solution(2726497459547294447)
XLA Ops:
  7.2 10.8 %all-gather = f32[256,128]{1,0:T(8,128)S(1)} all-gather(f32[64,128]{1,0:T(8,128)} %param.6), channel_id=2, replica_groups=mesh['row_0'=4,'row_1'=4,'row_2'=8,'col'=2] {'row_0'}, dimensions={0}, use_global_device_ids=true | all-gather | bytes 163840 | tf_op jit(solution)/shard_map/all_gather | solution.py:39
  18.0 11.0 %all_gather.10 = f32[16,64,128]{2,1,0:T(8,128)} all-gather(f32[4,64,128]{2,1,0:T(8,128)S(1)} %bitcast.79), channel_id=1, replica_groups=mesh['row_0'=4,'row_1'=4,'row_2'=8,'col'=2] {'row_1'}, dimensions={0}, use_global_device_ids=true | all-gather | bytes 655360 | tf_op jit(solution)/shard_map/all_gather | solution.py:39
  30.3 8.7 %psum.56 = f32[]{:T(128)} all-reduce(f32[]{:T(128)} %reduce_sum.144), channel_id=1, replica_groups=mesh['row_0'=4,'row_1'=4,'row_2'=8,'col'=2] {'row_0'}, use_global_device_ids=true, to_apply=%region_1.0 | all-reduce | flops 1 | bytes 8 | tf_op jit(solution)/shard_map/psum | solution.py:33
  39.0 9.2 %psum.57 = f32[]{:T(128)} all-reduce(f32[]{:T(128)} %psum.56), channel_id=1, replica_groups=mesh['row_0'=4,'row_1'=4,'row_2'=8,'col'=2] {'row_1'}, use_global_device_ids=true, to_apply=%region_2.0 | all-reduce | flops 1 | bytes 8 | tf_op jit(solution)/shard_map/psum | solution.py:33
  48.2 19.2 %psum.58 = f32[]{:T(128)} all-reduce(f32[]{:T(128)} %psum.57), channel_id=1, replica_groups=mesh['row_0'=4,'row_1'=4,'row_2'=8,'col'=2] {'row_2'}, use_global_device_ids=true, to_apply=%region_3.0 | all-reduce | flops 1 | bytes 8 | tf_op jit(solution)/shard_map/psum | solution.py:33
  68.8 15.1 %all-to-all-start = ((f32[2,64,128]{2,1,0:T(8,128)}), f32[2,64,128]{2,1,0:T(8,128)S(1)}, u32[]{:S(2)}, u32[]{:S(2)}) async-start(f32[2,64,128]{2,1,0:T(8,128)} %broadcast_in_dim.39), calls=%async_computation | async-start | bytes 131072 | tf_op jit(solution)/shard_map/all_to_all | solution.py:25
  88.9 3.3 all-to-all-start.1
  96.9 52.0 %while.22 = (s32[]{:T(128)}, f32[8,2048]{1,0:T(8,128)S(1)}, f32[8,256]{1,0:T(8,128)S(1)}, s32[8]{0:T(128)S(1)}, f32[64,16384]{1,0:T(8,128)}, /*index=5*/f32[64,2...) while((s32[]{:T(128)}, f32[8,2048]{1,0:T(8,128)S(1)}, ...), condition=%wide.region_7.8_spmd, body=%wide.region_5.7_spmd.sunk | while | flops 411565824 | bytes 4812979 | solution.py:102
  104.6 3.2 fusion.40
  117.6 3.2 fusion.40
  124.1 3.2 fusion.40
  130.6 3.2 fusion.40
  137.1 3.2 fusion.40
  143.6 3.2 fusion.40
  149.6 6.0 %all-to-all-start.2 = ((f32[32,4,128]{2,1,0:T(4,128)}), f32[32,4,128]{2,1,0:T(4,128)S(1)}, u32[]{:S(2)}, u32[]{:S(2)}) async-start(f32[32,4,128]{2,1,0:T(4,128)} %copy.25), calls=%async_computation.2 | async-start | bytes 131072 | tf_op jit(solution)/shard_map/all_to_all | solution.py:58
  156.2 8.3 %all-to-all-done.2 = f32[32,4,128]{2,1,0:T(4,128)S(1)} async-done(((f32[32,4,128]{2,1,0:T(4,128)}), f32[32,4,128]{2,1,0:T(4,128)S(1)}, u32[]{:S(2)}, u32[]{:S(2)}) %all-to-all-start.2) | async-done | bytes 65568 | tf_op jit(solution)/shard_map/all_to_all | solution.py:58
  164.5 5.4 %all-to-all-start.4 = ((f32[2,1,128]{2,1,0:T(1,128)}), f32[2,1,128]{2,1,0:T(1,128)S(1)}, u32[]{:S(2)}, u32[]{:S(2)}) async-start(f32[2,1,128]{2,1,0:T(1,128)} %bitcast.18), calls=%async_computation.4 | async-start | bytes 2048 | tf_op jit(solution)/shard_map/all_to_all | solution.py:58
  170.9 4.0 %all-to-all-start.3 = ((f32[4,1,128]{2,1,0:T(1,128)}), f32[4,1,128]{2,1,0:T(1,128)S(1)}, u32[]{:S(2)}, u32[]{:S(2)}) async-start(f32[4,1,128]{2,1,0:T(1,128)} %bitcast.17), calls=%async_computation.3 | async-start | bytes 4096 | tf_op jit(solution)/shard_map/all_to_all | solution.py:66
  174.9 4.0 %all-to-all-done.3 = f32[4,1,128]{2,1,0:T(1,128)S(1)} async-done(((f32[4,1,128]{2,1,0:T(1,128)}), f32[4,1,128]{2,1,0:T(1,128)S(1)}, u32[]{:S(2)}, u32[]{:S(2)}) %all-to-all-start.3) | async-done | bytes 2080 | tf_op jit(solution)/shard_map/all_to_all | solution.py:66
  181.5 5.9 %all-to-all-start.5 = ((f32[64,1,2]{2,1,0:T(1,128)}), f32[64,1,2]{2,1,0:T(1,128)S(1)}, u32[]{:S(2)}, u32[]{:S(2)}) async-start(f32[64,1,2]{2,1,0:T(1,128)} %broadcast_in_dim.42), calls=%async_computation.5 | async-start | bytes 65536 | tf_op jit(solution)/shard_map/all_to_all | solution.py:25
  187.4 9.4 %all-to-all-done.5 = f32[64,1,2]{2,1,0:T(1,128)S(1)} async-done(((f32[64,1,2]{2,1,0:T(1,128)}), f32[64,1,2]{2,1,0:T(1,128)S(1)}, u32[]{:S(2)}, u32[]{:S(2)}) %all-to-all-start.5) | async-done | bytes 544 | tf_op jit(solution)/shard_map/all_to_all | solution.py:25
  196.9 6.5 %all_to_all.78 = f32[4,1,2]{2,1,0:T(1,128)S(1)} all-to-all(f32[4,1,2]{2,1,0:T(1,128)S(1)} %broadcast_in_dim.43), channel_id=1, replica_groups=mesh['row_0'=4,'row_1'=4,'row_2'=8,'col'=2] {'row_0'}, dimensions={0} | all-to-all | bytes 64 | tf_op jit(solution)/shard_map/all_to_all | solution.py:25
  204.7 5.2 %all_to_all.79 = f32[2,1,128]{2,1,0:T(1,128)S(1)} all-to-all(f32[2,1,128]{2,1,0:T(1,128)S(1)} %broadcast_in_dim.44), channel_id=1, replica_groups=mesh['row_0'=4,'row_1'=4,'row_2'=8,'col'=2] {'col'}, dimensions={0} | all-to-all | bytes 2048 | tf_op jit(solution)/shard_map/all_to_all | solution.py:25
  209.9 51.2 %while.23 = (s32[]{:T(128)}, f32[8,2048]{1,0:T(8,128)S(1)}, s32[8]{0:T(128)S(1)}, f32[64,16384]{1,0:T(8,128)}, f32[64,256]{1,0:T(8,128)S(1)}, /*index=5*/f32[256...) while((s32[]{:T(128)}, f32[8,2048]{1,0:T(8,128)S(1)}, s32[8]{0:T(128)S(1)}, ...), condition=%wide.region_16.17_spmd, body=%wide.region_15.16_spmd.sunk | while | flops 411041792 | bytes 4809895 | solution.py:102
  261.2 11.8 %all_to_all.81 = f32[32,4,128]{2,1,0:T(4,128)S(1)} all-to-all(f32[32,4,128]{2,1,0:T(4,128)S(1)} %copy.29), channel_id=1, replica_groups=mesh['row_0'=4,'row_1'=4,'row_2'=8,'col'=2] {'row_1','row_2'}, dimensions={0} | all-to-all | bytes 131072 | tf_op jit(solution)/shard_map/all_to_all | solution.py:58
  273.1 6.5 %all_to_all.82 = f32[4,1,128]{2,1,0:T(1,128)S(1)} all-to-all(f32[4,1,128]{2,1,0:T(1,128)S(1)} %bitcast.88), channel_id=1, replica_groups=mesh['row_0'=4,'row_1'=4,'row_2'=8,'col'=2] {'row_0'}, dimensions={0} | all-to-all | bytes 4096 | tf_op jit(solution)/shard_map/all_to_all | solution.py:66
  281.6 15.4 %all_to_all.83 = f32[64,1,2]{2,1,0:T(1,128)S(1)} all-to-all(f32[64,1,2]{2,1,0:T(1,128)S(1)} %broadcast_in_dim.45), channel_id=1, replica_groups=mesh['row_0'=4,'row_1'=4,'row_2'=8,'col'=2] {'row_1','row_2','col'}, dimensions={0} | all-to-all | bytes 1024 | tf_op jit(solution)/shard_map/all_to_all | solution.py:25
  297.0 6.5 %all_to_all.80 = f32[4,1,2]{2,1,0:T(1,128)S(1)} all-to-all(f32[4,1,2]{2,1,0:T(1,128)S(1)} %broadcast_in_dim.46), channel_id=1, replica_groups=mesh['row_0'=4,'row_1'=4,'row_2'=8,'col'=2] {'row_0'}, dimensions={0} | all-to-all | bytes 64 | tf_op jit(solution)/shard_map/all_to_all | solution.py:25
  305.4 7.5 %psum.60 = f32[]{:T(128)} all-reduce(f32[]{:T(128)} %get-tuple-element.101), channel_id=1, replica_groups=mesh['row_0'=4,'row_1'=4,'row_2'=8,'col'=2] {'row_0'}, use_global_device_ids=true, to_apply=%region_24.25 | all-reduce | flops 1 | bytes 8 | tf_op jit(solution)/shard_map/psum | solution.py:33
  312.9 7.4 %psum.61 = f32[]{:T(128)} all-reduce(f32[]{:T(128)} %psum.60), channel_id=1, replica_groups=mesh['row_0'=4,'row_1'=4,'row_2'=8,'col'=2] {'row_1'}, use_global_device_ids=true, to_apply=%region_25.26 | all-reduce | flops 1 | bytes 8 | tf_op jit(solution)/shard_map/psum | solution.py:33
  320.3 11.6 %psum.62 = f32[]{:T(128)} all-reduce(f32[]{:T(128)} %psum.61), channel_id=1, replica_groups=mesh['row_0'=4,'row_1'=4,'row_2'=8,'col'=2] {'row_2'}, use_global_device_ids=true, to_apply=%region_26.27 | all-reduce | flops 1 | bytes 8 | tf_op jit(solution)/shard_map/psum | solution.py:33
  331.9 12.3 %psum.63 = f32[1]{0:T(128)} all-reduce(f32[1]{0:T(128)} %bitcast.28), channel_id=1, replica_groups=mesh['row_0'=4,'row_1'=4,'row_2'=8,'col'=2] {'col'}, use_global_device_ids=true, to_apply=%region_27.28 | all-reduce | flops 1 | bytes 8 | tf_op jit(solution)/shard_map/psum | solution.py:33
  (117 shorter events, 98.8 us)
Async XLA Ops:
  7.2 85.0 %all-gather.3.cloned.1.call-start = ((), (), s32[]{:S(2)}) async-start(), calls=%async_computation.12 | async-start | bytes 4718592 | tf_op jit(solution)/shard_map/all_gather | solution.py:39
  68.8 19.5 %all-to-all-start = ((f32[2,64,128]{2,1,0:T(8,128)}), f32[2,64,128]{2,1,0:T(8,128)S(1)}, u32[]{:S(2)}, u32[]{:S(2)}) async-start(f32[2,64,128]{2,1,0:T(8,128)} %broadcast_in_dim.39), calls=%async_computation | async-start | bytes 131072 | tf_op jit(solution)/shard_map/all_to_all | solution.py:25
  88.9 8.0 %all-to-all-start.1 = ((f32[2,1,128]{2,1,0:T(1,128)}), f32[2,1,128]{2,1,0:T(1,128)S(1)}, u32[]{:S(2)}, u32[]{:S(2)}) async-start(f32[2,1,128]{2,1,0:T(1,128)} %broadcast_in_dim.41), calls=%async_computation.1 | async-start | bytes 2048 | tf_op jit(solution)/shard_map/all_to_all | solution.py:25
  96.9 82.0 %copy-start = (f32[128]{0:T(128)S(1)}, f32[128]{0:T(128)}, u32[]{:S(2)}) copy-start(f32[128]{0:T(128)} %param.7) | copy-start | bytes 1540
  149.6 14.9 %all-to-all-start.2 = ((f32[32,4,128]{2,1,0:T(4,128)}), f32[32,4,128]{2,1,0:T(4,128)S(1)}, u32[]{:S(2)}, u32[]{:S(2)}) async-start(f32[32,4,128]{2,1,0:T(4,128)} %copy.25), calls=%async_computation.2 | async-start | bytes 131072 | tf_op jit(solution)/shard_map/all_to_all | solution.py:58
  164.5 6.4 %all-to-all-start.4 = ((f32[2,1,128]{2,1,0:T(1,128)}), f32[2,1,128]{2,1,0:T(1,128)S(1)}, u32[]{:S(2)}, u32[]{:S(2)}) async-start(f32[2,1,128]{2,1,0:T(1,128)} %bitcast.18), calls=%async_computation.4 | async-start | bytes 2048 | tf_op jit(solution)/shard_map/all_to_all | solution.py:58
  170.9 8.0 %all-to-all-start.3 = ((f32[4,1,128]{2,1,0:T(1,128)}), f32[4,1,128]{2,1,0:T(1,128)S(1)}, u32[]{:S(2)}, u32[]{:S(2)}) async-start(f32[4,1,128]{2,1,0:T(1,128)} %bitcast.17), calls=%async_computation.3 | async-start | bytes 4096 | tf_op jit(solution)/shard_map/all_to_all | solution.py:66
  181.5 15.3 %all-to-all-start.5 = ((f32[64,1,2]{2,1,0:T(1,128)}), f32[64,1,2]{2,1,0:T(1,128)S(1)}, u32[]{:S(2)}, u32[]{:S(2)}) async-start(f32[64,1,2]{2,1,0:T(1,128)} %broadcast_in_dim.42), calls=%async_computation.5 | async-start | bytes 65536 | tf_op jit(solution)/shard_map/all_to_all | solution.py:25
Sparse Core Ops, SparseCore 0:
  29.2 62.1 all-gather.2
where the time goes:
time: 355 us; the launch traced here: 353 us
  blocking collectives  153 us (43%)
  matrix products  79.7 us (22%)
  starting transfers between devices  39.7 us (11%)
  waiting for transfers between devices  22.1 us (6%)
  local copies, waits for them, and re-layouts  21.5 us (6%)
  between operations  14.1 us (4%)
  other arithmetic  12.9 us (4%)
  loops' own time  10.7 us (3%)
    psum x8, blocking collectives, one_axis_at_a_time(): return functools.reduce(lax.psum, axes, array)  79 us
    dot_general x16, matrix products, one_block(): jnp.einsum('kr,kc->rc', row_side, segment, precision=lax.Precision.HIGHEST)  50 us
    all_to_all x4, blocking collectives, copy_for_each(): return lax.all_to_all(copies, axis, split_axis=0, concat_axis=0, tiled=True)  33.5 us
    dot_general x16, matrix products, one_block(): inflow = jnp.dot(rows_mass, moves, precision=lax.Precision.HIGHEST)  29.7 us
    all_to_all x3, starting transfers between devices, copy_for_each(): return lax.all_to_all(copies, axis, split_axis=0, concat_axis=0, tiled=True)  24.3 us
    all_gather x2, blocking collectives, all_blocks(): blocks = lax.all_gather(blocks, axes[k], axis=0, tiled=True)  21.8 us
    all_to_all x1, blocking collectives, sum_at_owner(): lax.all_to_all(blocks, axis, split_axis=0, concat_axis=0, tiled=True)  11.8 us
    all_to_all x2, starting transfers between devices, sum_at_owner(): lax.all_to_all(blocks, axis, split_axis=0, concat_axis=0, tiled=True)  11.4 us
  transfers between devices with their start and end apart: 7, of which 4 were waited for; matrix products, arithmetic and copies ran while one was open for 3% of the time, Pallas kernels for 0%

commit v1 on v0

--- a/solution.py
+++ b/solution.py
@@ -36,7 +36,9 @@
 def all_blocks(array, axes, turns):
     blocks = array[None]
     for k in turns:
-        blocks = lax.all_gather(blocks, axes[k], axis=0, tiled=True)
+        blocks = jnp.concatenate(
+            lax.all_to_all(jnp.stack([blocks] * lax.axis_size(axes[k])), axes[k], 0, 0), axis=0
+        )
     block = [lax.axis_size(axes[k]) for k in reversed(turns)]
     blocks = blocks.reshape(*block, *array.shape)
     turned = sorted(range(len(turns)), key=lambda place: turns[len(turns) - 1 - place])

time: 355 us -> 405 us (1.14)
  blocking collectives: 153 us -> 222 us
  between operations: 14.1 us -> 0.78 us
  starting transfers between devices: 39.7 us -> 31.8 us
    psum x8, blocking collectives: 79 us -> 145 us  [one_axis_at_a_time(): return functools.reduce(lax.psum, axes, array)]
    all_gather x2 -> x0, blocking collectives: 21.8 us -> none  [all_blocks(): blocks = lax.all_gather(blocks, axes[k], axis=0, tiled=True)]
    all_to_all x0 -> x2, blocking collectives: none -> 18.1 us  [all_blocks(): lax.all_to_all(jnp.stack([blocks] * lax.axis_size(axes[k])), axes[k], 0, 0)]
    all_to_all x3 -> x2, starting transfers between devices: 24.3 us -> 9.09 us  [copy_for_each(): return lax.all_to_all(copies, axis, split_axis=0, concat_axis=0, tiled=True)]
    all_to_all x0 -> x1, starting transfers between devices: none -> 8.32 us  [all_blocks(): lax.all_to_all(jnp.stack([blocks] * lax.axis_size(axes[k])), axes[k], 0, 0)]
    all_to_all x4 -> x5, blocking collectives: 33.5 us -> 40.1 us  [copy_for_each(): return lax.all_to_all(copies, axis, split_axis=0, concat_axis=0, tiled=True)]
    all_to_all x3 -> x2, waiting for transfers between devices: 9.43 us -> 9.43 us  [copy_for_each(): return lax.all_to_all(copies, axis, split_axis=0, concat_axis=0, tiled=True)]
  transfers between devices with their start and end apart: 7 -> 6, of which waited for: 4 -> 4; matrix products, arithmetic and copies ran while one was open for 3% -> 2% of each run, Pallas kernels for 0% -> 0%
where the time goes in v1:
time: 405 us; the launch traced here: 403 us
  blocking collectives  222 us (55%)
  matrix products  79.7 us (20%)
  starting transfers between devices  31.8 us (8%)
  local copies, waits for them, and re-layouts  24.2 us (6%)
  waiting for transfers between devices  22 us (5%)
  other arithmetic  11.6 us (3%)
  loops' own time  10.7 us (3%)
    psum x8, blocking collectives, one_axis_at_a_time(): return functools.reduce(lax.psum, axes, array)  145 us
    dot_general x16, matrix products, one_block(): jnp.einsum('kr,kc->rc', row_side, segment, precision=lax.Precision.HIGHEST)  50 us
    all_to_all x5, blocking collectives, copy_for_each(): return lax.all_to_all(copies, axis, split_axis=0, concat_axis=0, tiled=True)  40.1 us
    dot_general x16, matrix products, one_block(): inflow = jnp.dot(rows_mass, moves, precision=lax.Precision.HIGHEST)  29.7 us
    all_to_all x2, blocking collectives, all_blocks(): lax.all_to_all(jnp.stack([blocks] * lax.axis_size(axes[k])), axes[k], 0, 0)  18.1 us
    all_to_all x1, blocking collectives, sum_at_owner(): lax.all_to_all(blocks, axis, split_axis=0, concat_axis=0, tiled=True)  11.8 us
    all_to_all x2, starting transfers between devices, sum_at_owner(): lax.all_to_all(blocks, axis, split_axis=0, concat_axis=0, tiled=True)  11.2 us
    another operation x2, loops' own time, column_pass(): lax.map(one_block, jnp.arange(count_blocks, dtype=jnp.int32))  10.7 us
  transfers between devices with their start and end apart: 6, of which 4 were waited for; matrix products, arithmetic and copies ran while one was open for 2% of the time, Pallas kernels for 0%

profile of v1, /device:TPU:1, one launch (start us, length us, event | category | flops | bytes accessed | tf_op | source)
XLA Modules:
  0.0 402.8 jit_solution(8859816821359746671)
XLA Ops:
  1.4 6.6 %all_to_all.93 = f32[2,64,128]{2,1,0:T(8,128)S(1)} all-to-all(f32[2,64,128]{2,1,0:T(8,128)S(1)} %broadcast_in_dim.35), channel_id=1, replica_groups=mesh['row_0'=4,'row_1'=4,'row_2'=8,'col'=2] {'col'}, dimensions={0} | all-to-all | bytes 131072 | tf_op jit(solution)/shard_map/all_to_all | solution.py:25
  8.8 7.2 %all_to_all.94 = f32[4,1,64,128]{3,2,1,0:T(8,128)S(1)} all-to-all(f32[4,1,64,128]{3,2,1,0:T(8,128)S(1)} %stack.15), channel_id=1, replica_groups=mesh['row_0'=4,'row_1'=4,'row_2'=8,'col'=2] {'row_0'}, dimensions={0} | all-to-all | bytes 262144 | tf_op jit(solution)/shard_map/all_to_all | solution.py:40
  16.1 10.9 %all_to_all.95 = f32[4,4,64,128]{3,2,1,0:T(8,128)S(1)} all-to-all(f32[4,4,64,128]{3,2,1,0:T(8,128)S(1)} %stack.16), channel_id=1, replica_groups=mesh['row_0'=4,'row_1'=4,'row_2'=8,'col'=2] {'row_1'}, dimensions={0} | all-to-all | bytes 1048576 | tf_op jit(solution)/shard_map/all_to_all | solution.py:40
  29.5 8.3 %all-to-all-start.2 = ((f32[8,16,64,128]{3,2,1,0:T(8,128)}), f32[8,16,64,128]{3,2,1,0:T(8,128)}, u32[]{:S(2)}, u32[]{:S(2)}) async-start(f32[8,16,64,128]{3,2,1,0:T(8,128)} %stack.17), calls=%async_computation.2 | async-start | bytes 8388608 | tf_op jit(solution)/shard_map/all_to_all | solution.py:40
  38.4 7.5 %psum.56 = f32[]{:T(128)} all-reduce(f32[]{:T(128)} %reduce_sum.144), channel_id=1, replica_groups=mesh['row_0'=4,'row_1'=4,'row_2'=8,'col'=2] {'row_0'}, use_global_device_ids=true, to_apply=%region_1.0 | all-reduce | flops 1 | bytes 8 | tf_op jit(solution)/shard_map/psum | solution.py:33
  45.9 8.3 %psum.57 = f32[]{:T(128)} all-reduce(f32[]{:T(128)} %psum.56), channel_id=1, replica_groups=mesh['row_0'=4,'row_1'=4,'row_2'=8,'col'=2] {'row_1'}, use_global_device_ids=true, to_apply=%region_2.0 | all-reduce | flops 1 | bytes 8 | tf_op jit(solution)/shard_map/psum | solution.py:33
  54.2 82.7 %psum.58 = f32[]{:T(128)} all-reduce(f32[]{:T(128)} %psum.57), channel_id=1, replica_groups=mesh['row_0'=4,'row_1'=4,'row_2'=8,'col'=2] {'row_2'}, use_global_device_ids=true, to_apply=%region_3.0 | all-reduce | flops 1 | bytes 8 | tf_op jit(solution)/shard_map/psum | solution.py:33
  136.9 8.0 %psum.59 = f32[]{:T(128)} all-reduce(f32[]{:T(128)} %psum.58), channel_id=1, replica_groups=mesh['row_0'=4,'row_1'=4,'row_2'=8,'col'=2] {'col'}, use_global_device_ids=true, to_apply=%region_4.0 | all-reduce | flops 1 | bytes 8 | tf_op jit(solution)/shard_map/psum | solution.py:33
  146.2 3.5 all-to-all-start.4
  154.4 52.0 %while.22 = (s32[]{:T(128)}, f32[8,2048]{1,0:T(8,128)S(1)}, f32[8,256]{1,0:T(8,128)S(1)}, s32[8]{0:T(128)S(1)}, f32[64,16384]{1,0:T(8,128)}, /*index=5*/f32[64,2...) while((s32[]{:T(128)}, f32[8,2048]{1,0:T(8,128)S(1)}, ...), condition=%wide.region_7.8_spmd, body=%wide.region_5.7_spmd.sunk | while | flops 411565824 | bytes 4812979 | solution.py:104
  162.1 3.2 fusion.40
  175.1 3.2 fusion.40
  181.6 3.2 fusion.40
  194.6 3.2 fusion.40
  207.1 6.6 %all-to-all-start.5 = ((f32[32,4,128]{2,1,0:T(4,128)}), f32[32,4,128]{2,1,0:T(4,128)S(1)}, u32[]{:S(2)}, u32[]{:S(2)}) async-start(f32[32,4,128]{2,1,0:T(4,128)} %copy.25), calls=%async_computation.5 | async-start | bytes 131072 | tf_op jit(solution)/shard_map/all_to_all | solution.py:60
  214.3 8.3 %all-to-all-done.5 = f32[32,4,128]{2,1,0:T(4,128)S(1)} async-done(((f32[32,4,128]{2,1,0:T(4,128)}), f32[32,4,128]{2,1,0:T(4,128)S(1)}, u32[]{:S(2)}, u32[]{:S(2)}) %all-to-all-start.5) | async-done | bytes 65568 | tf_op jit(solution)/shard_map/all_to_all | solution.py:60
  222.6 4.6 %all-to-all-start.7 = ((f32[2,1,128]{2,1,0:T(1,128)}), f32[2,1,128]{2,1,0:T(1,128)S(1)}, u32[]{:S(2)}, u32[]{:S(2)}) async-start(f32[2,1,128]{2,1,0:T(1,128)} %bitcast.19), calls=%async_computation.7 | async-start | bytes 2048 | tf_op jit(solution)/shard_map/all_to_all | solution.py:60
  228.2 3.2 all-to-all-start.6
  231.4 3.9 all-to-all-done.6
  237.9 5.6 %all-to-all-start.8 = ((f32[64,1,2]{2,1,0:T(1,128)}), f32[64,1,2]{2,1,0:T(1,128)S(1)}, u32[]{:S(2)}, u32[]{:S(2)}) async-start(f32[64,1,2]{2,1,0:T(1,128)} %broadcast_in_dim.38), calls=%async_computation.8 | async-start | bytes 65536 | tf_op jit(solution)/shard_map/all_to_all | solution.py:25
  243.6 9.4 %all-to-all-done.8 = f32[64,1,2]{2,1,0:T(1,128)S(1)} async-done(((f32[64,1,2]{2,1,0:T(1,128)}), f32[64,1,2]{2,1,0:T(1,128)S(1)}, u32[]{:S(2)}, u32[]{:S(2)}) %all-to-all-start.8) | async-done | bytes 544 | tf_op jit(solution)/shard_map/all_to_all | solution.py:25
  253.1 6.5 %all_to_all.96 = f32[4,1,2]{2,1,0:T(1,128)S(1)} all-to-all(f32[4,1,2]{2,1,0:T(1,128)S(1)} %broadcast_in_dim.39), channel_id=1, replica_groups=mesh['row_0'=4,'row_1'=4,'row_2'=8,'col'=2] {'row_0'}, dimensions={0} | all-to-all | bytes 64 | tf_op jit(solution)/shard_map/all_to_all | solution.py:25
  260.9 5.2 %all_to_all.97 = f32[2,1,128]{2,1,0:T(1,128)S(1)} all-to-all(f32[2,1,128]{2,1,0:T(1,128)S(1)} %broadcast_in_dim.40), channel_id=1, replica_groups=mesh['row_0'=4,'row_1'=4,'row_2'=8,'col'=2] {'col'}, dimensions={0} | all-to-all | bytes 2048 | tf_op jit(solution)/shard_map/all_to_all | solution.py:25
  266.0 51.3 %while.23 = (s32[]{:T(128)}, f32[8,2048]{1,0:T(8,128)S(1)}, s32[8]{0:T(128)S(1)}, f32[64,16384]{1,0:T(8,128)}, f32[64,256]{1,0:T(8,128)S(1)}, /*index=5*/f32[256...) while((s32[]{:T(128)}, f32[8,2048]{1,0:T(8,128)S(1)}, s32[8]{0:T(128)S(1)}, ...), condition=%wide.region_16.17_spmd, body=%wide.region_15.16_spmd.sunk | while | flops 411041792 | bytes 4809895 | solution.py:104
  317.4 11.8 %all_to_all.99 = f32[32,4,128]{2,1,0:T(4,128)S(1)} all-to-all(f32[32,4,128]{2,1,0:T(4,128)S(1)} %copy.29), channel_id=1, replica_groups=mesh['row_0'=4,'row_1'=4,'row_2'=8,'col'=2] {'row_1','row_2'}, dimensions={0} | all-to-all | bytes 131072 | tf_op jit(solution)/shard_map/all_to_all | solution.py:60
  329.2 6.5 %all_to_all.100 = f32[4,1,128]{2,1,0:T(1,128)S(1)} all-to-all(f32[4,1,128]{2,1,0:T(1,128)S(1)} %bitcast.89), channel_id=1, replica_groups=mesh['row_0'=4,'row_1'=4,'row_2'=8,'col'=2] {'row_0'}, dimensions={0} | all-to-all | bytes 4096 | tf_op jit(solution)/shard_map/all_to_all | solution.py:68
  337.7 15.4 %all_to_all.101 = f32[64,1,2]{2,1,0:T(1,128)S(1)} all-to-all(f32[64,1,2]{2,1,0:T(1,128)S(1)} %broadcast_in_dim.41), channel_id=1, replica_groups=mesh['row_0'=4,'row_1'=4,'row_2'=8,'col'=2] {'row_1','row_2','col'}, dimensions={0} | all-to-all | bytes 1024 | tf_op jit(solution)/shard_map/all_to_all | solution.py:25
  353.2 6.5 %all_to_all.98 = f32[4,1,2]{2,1,0:T(1,128)S(1)} all-to-all(f32[4,1,2]{2,1,0:T(1,128)S(1)} %broadcast_in_dim.42), channel_id=1, replica_groups=mesh['row_0'=4,'row_1'=4,'row_2'=8,'col'=2] {'row_0'}, dimensions={0} | all-to-all | bytes 64 | tf_op jit(solution)/shard_map/all_to_all | solution.py:25
  361.6 7.5 %psum.60 = f32[]{:T(128)} all-reduce(f32[]{:T(128)} %get-tuple-element.101), channel_id=1, replica_groups=mesh['row_0'=4,'row_1'=4,'row_2'=8,'col'=2] {'row_0'}, use_global_device_ids=true, to_apply=%region_24.25 | all-reduce | flops 1 | bytes 8 | tf_op jit(solution)/shard_map/psum | solution.py:33
  369.1 7.4 %psum.61 = f32[]{:T(128)} all-reduce(f32[]{:T(128)} %psum.60), channel_id=1, replica_groups=mesh['row_0'=4,'row_1'=4,'row_2'=8,'col'=2] {'row_1'}, use_global_device_ids=true, to_apply=%region_25.26 | all-reduce | flops 1 | bytes 8 | tf_op jit(solution)/shard_map/psum | solution.py:33
  376.4 11.6 %psum.62 = f32[]{:T(128)} all-reduce(f32[]{:T(128)} %psum.61), channel_id=1, replica_groups=mesh['row_0'=4,'row_1'=4,'row_2'=8,'col'=2] {'row_2'}, use_global_device_ids=true, to_apply=%region_26.27 | all-reduce | flops 1 | bytes 8 | tf_op jit(solution)/shard_map/psum | solution.py:33
  388.1 12.3 %psum.63 = f32[1]{0:T(128)} all-reduce(f32[1]{0:T(128)} %bitcast.29), channel_id=1, replica_groups=mesh['row_0'=4,'row_1'=4,'row_2'=8,'col'=2] {'col'}, use_global_device_ids=true, to_apply=%region_27.28 | all-reduce | flops 1 | bytes 8 | tf_op jit(solution)/shard_map/psum | solution.py:33
  (118 shorter events, 103.3 us)
Async XLA Ops:
  29.5 8.3 %copy-start = (f32[128]{0:T(128)S(1)}, f32[128]{0:T(128)}, u32[]{:S(2)}) copy-start(f32[128]{0:T(128)} %param.7) | copy-start | bytes 1540
  29.5 116.1 %all-to-all-start.2 = ((f32[8,16,64,128]{3,2,1,0:T(8,128)}), f32[8,16,64,128]{3,2,1,0:T(8,128)}, u32[]{:S(2)}, u32[]{:S(2)}) async-start(f32[8,16,64,128]{3,2,1,0:T(8,128)} %stack.17), calls=%async_computation.2 | async-start | bytes 8388608 | tf_op jit(solution)/shard_map/all_to_all | solution.py:40
  146.2 8.2 %all-to-all-start.4 = ((f32[2,1,128]{2,1,0:T(1,128)}), f32[2,1,128]{2,1,0:T(1,128)S(1)}, u32[]{:S(2)}, u32[]{:S(2)}) async-start(f32[2,1,128]{2,1,0:T(1,128)} %broadcast_in_dim.37), calls=%async_computation.4 | async-start | bytes 2048 | tf_op jit(solution)/shard_map/all_to_all | solution.py:25
  207.1 15.5 %all-to-all-start.5 = ((f32[32,4,128]{2,1,0:T(4,128)}), f32[32,4,128]{2,1,0:T(4,128)S(1)}, u32[]{:S(2)}, u32[]{:S(2)}) async-start(f32[32,4,128]{2,1,0:T(4,128)} %copy.25), calls=%async_computation.5 | async-start | bytes 131072 | tf_op jit(solution)/shard_map/all_to_all | solution.py:60
  222.6 5.6 %all-to-all-start.7 = ((f32[2,1,128]{2,1,0:T(1,128)}), f32[2,1,128]{2,1,0:T(1,128)S(1)}, u32[]{:S(2)}, u32[]{:S(2)}) async-start(f32[2,1,128]{2,1,0:T(1,128)} %bitcast.19), calls=%async_computation.7 | async-start | bytes 2048 | tf_op jit(solution)/shard_map/all_to_all | solution.py:60
  228.2 7.1 %all-to-all-start.6 = ((f32[4,1,128]{2,1,0:T(1,128)}), f32[4,1,128]{2,1,0:T(1,128)S(1)}, u32[]{:S(2)}, u32[]{:S(2)}) async-start(f32[4,1,128]{2,1,0:T(1,128)} %bitcast.18), calls=%async_computation.6 | async-start | bytes 4096 | tf_op jit(solution)/shard_map/all_to_all | solution.py:68
  237.9 15.1 %all-to-all-start.8 = ((f32[64,1,2]{2,1,0:T(1,128)}), f32[64,1,2]{2,1,0:T(1,128)S(1)}, u32[]{:S(2)}, u32[]{:S(2)}) async-start(f32[64,1,2]{2,1,0:T(1,128)} %broadcast_in_dim.38), calls=%async_computation.8 | async-start | bytes 65536 | tf_op jit(solution)/shard_map/all_to_all | solution.py:25
